TPU v7x, 256 devices: a whole 4x4x8 slice. The times are simulated.
256 devices in a mesh: dp: 8 (over z), expert: 32 (over x, y, core).
Axes of the slice: x: 4, y: 4, z: 8, core: 2. Of those that a mesh axis runs over, the one named last changes fastest.
Arguments:
- tokens: bfloat16 [65536, 2048], P(('dp', 'expert')), may hold values from -6 to 6
- expert_ranks: int32 [32, 65536], P(None, ('dp', 'expert')), may hold values from 0 to 65535, as said below
- capacity: int32 [32], replicated, may hold values from 512 to 1024, as said below
- weight_in: bfloat16 [32, 2048, 8192], P('expert', None, 'dp'), may hold values from -0.125 to 0.125
- weight_out: bfloat16 [32, 8192, 2048], P('expert', 'dp'), may hold values from -0.0625 to 0.0625
- gate_weights: float32 [32, 1024], P('expert', 'dp'), may hold values from 0.05 to 1
Outputs:
- combined: bfloat16 [65536, 2048], P(('dp', 'expert'))
Inputs may be any that keep to these rules, and one draw needn't show every extreme that they name: `expert_ranks`: for each expert the ranks are a permutation of 0 to 65535. Of the 256 tokens of one device, at most 8 have rank under 1024 for one expert; for an expert of capacity 1024, some devices have exactly 8. At least one expert has capacity 1024.
All inputs are finite; a program needn't handle non-finite values.
Results may differ from a plain program's by a relative error of at most 0.0053.
Values may be sent and summed in bfloat16 or wider, within the bound.
No kernel may reach another device: no remote copies, remote signals or barrier semaphores. Data moves between devices by JAX's collectives and lax.ppermute only.
A program may use at most 64 MiB of HBM per device.

v0:
```python
import jax
import jax.numpy as jnp
from jax import lax
from jax.sharding import Mesh
from jax.sharding import PartitionSpec as P

MOST = 8
EXPERT = ("expert_0", "expert_1", "expert_2")
DP_EXPERT = ("dp", "expert_0", "expert_1", "expert_2")


def exclusive(values):
    return jnp.cumsum(values) - values


def on_device(tokens, expert_ranks, capacity, weight_in, weight_out, gate_weights):
    dp_count = lax.axis_size("dp")
    expert_count = lax.axis_size(EXPERT)
    token_count, width = tokens.shape
    slots_dp = gate_weights.shape[1]
    rows_all = expert_count * MOST
    own_dp = lax.axis_index("dp")
    own_expert = lax.axis_index(EXPERT)
    chosen = expert_ranks < capacity[:, None]
    chosen_int = chosen.astype(jnp.int32)
    counts = jnp.sum(chosen_int, axis=1)
    before = jnp.cumsum(chosen_int, axis=1) - chosen_int
    places = lax.broadcasted_iota(jnp.int32, (expert_count, MOST, token_count), 1)
    pack_table = jnp.logical_and(chosen[:, None, :], before[:, None, :] == places)
    pack_table = pack_table.astype(jnp.bfloat16).reshape(rows_all, token_count)
    packed = jnp.dot(pack_table, tokens, preferred_element_type=jnp.float32).astype(jnp.bfloat16)
    arrived_rows = lax.all_to_all(
        packed.reshape(expert_count, MOST, width), EXPERT, split_axis=0, concat_axis=0, tiled=True
    ).reshape(rows_all, width)
    device_ids = lax.broadcasted_iota(jnp.int32, (expert_count, expert_count), 0)
    expert_ids = lax.broadcasted_iota(jnp.int32, (expert_count, expert_count), 1)
    table = lax.psum(jnp.where(device_ids == own_expert, counts[None, :], 0), EXPERT)
    plane_ids = lax.broadcasted_iota(jnp.int32, (dp_count, expert_count), 0)
    plane_counts = lax.psum(
        jnp.where(plane_ids == own_dp, jnp.sum(table, axis=0)[None, :], 0), "dp"
    )
    most_rows = jnp.max(plane_counts)
    arrived = jnp.sum(jnp.where(expert_ids == own_expert, table, 0), axis=1)
    earlier = jnp.logical_and(plane_ids < own_dp, expert_ids[:dp_count] == own_expert)
    first_slot = jnp.sum(jnp.where(earlier, plane_counts, 0))
    within = lax.broadcasted_iota(jnp.int32, (expert_count, MOST), 1)
    target = jnp.where(within < arrived[:, None], exclusive(arrived)[:, None] + within, -1).reshape(
        rows_all
    )
    gates_all = lax.all_gather(gate_weights[0], "dp", axis=0, tiled=True)
    gates_all = jnp.concatenate([gates_all, jnp.zeros((rows_all,), gates_all.dtype)])

    def experts(rows, plane_rows):
        slot_ids = lax.broadcasted_iota(jnp.int32, (rows_all, plane_rows), 1)
        place_table = (target[:, None] == slot_ids).astype(jnp.bfloat16)
        plane = lax.dot_general(
            place_table, rows, (((0,), (0,)), ((), ())), preferred_element_type=jnp.float32
        ).astype(jnp.bfloat16)
        slot_rows = lax.all_gather(plane, "dp", axis=0, tiled=True)
        hidden = jnp.maximum(
            jnp.dot(slot_rows, weight_in[0], preferred_element_type=jnp.float32), 0.0
        ).astype(jnp.bfloat16)
        share = jnp.dot(hidden, weight_out[0], preferred_element_type=jnp.float32)
        out = lax.psum_scatter(
            share.astype(jnp.bfloat16), "dp", scatter_dimension=0, tiled=True
        ).astype(jnp.float32)
        gates = lax.dynamic_slice_in_dim(gates_all, first_slot, plane_rows, 0)
        scaled = (gates[:, None] * out).astype(jnp.bfloat16)
        returned = jnp.dot(place_table, scaled, preferred_element_type=jnp.float32)
        return returned.astype(jnp.bfloat16)

    fair = slots_dp + slots_dp // 4
    sent_back = lax.cond(
        most_rows <= fair,
        lambda rows: experts(rows, fair),
        lambda rows: experts(rows, rows_all),
        arrived_rows,
    )
    results = lax.all_to_all(
        sent_back.reshape(expert_count, MOST, width),
        EXPERT,
        split_axis=0,
        concat_axis=0,
        tiled=True,
    ).reshape(rows_all, width)
    combined = lax.dot_general(
        pack_table, results, (((0,), (0,)), ((), ())), preferred_element_type=jnp.float32
    )
    return combined.astype(jnp.bfloat16)


def solution(mesh):
    split = Mesh(
        mesh.devices.reshape(mesh.shape["dp"], 4, 4, 2), ("dp", "expert_0", "expert_1", "expert_2")
    )
    placed = (
        P(DP_EXPERT, None),
        P(None, DP_EXPERT),
        P(),
        P(EXPERT, None, "dp"),
        P(EXPERT, "dp", None),
        P(EXPERT, "dp"),
    )
    return jax.shard_map(
        on_device, mesh=split, in_specs=placed, out_specs=P(DP_EXPERT, None), check_vma=False
    )
```

profile of v0, /device:TPU:1, one launch (start us, length us, event | category | flops | bytes accessed | tf_op | source)
XLA Modules:
  0.0 359.8 jit_solution(15286796204240877624)
XLA Ops:
  6.5 0.9 convert_bitcast_fusion.1
  7.5 0.6 reduce-window.11
  8.1 0.2 slice_reduce_fusion
  8.3 0.1 iota.68
  8.4 0.1 convert_subtract_fusion
  8.5 1.5 fusion.21
  10.0 8.6 %all-to-all-start = ((bf16[32,8,2048]{2,1,0:T(8,128)(2,1)}), bf16[32,8,2048]{2,1,0:T(8,128)(2,1)S(1)}, u32[]{:S(2)}, u32[]{:S(2)}) async-start(bf16[32,8,2048]{2,1,0:T(8,128)(2,1)} %fusion.21), calls=%async_computation.2 | async-start | bytes 2097152 | tf_op jit(solution)/shard_map/all_to_all | solution.py:32
  18.7 127.2 %psum.14 = s32[32,32]{1,0:T(8,128)S(1)} all-reduce(s32[32,32]{1,0:T(8,128)S(1)} %broadcast_select_fusion), channel_id=1, replica_groups=mesh['dp'=8,'expert_0'=4,'expert_1'=4,'expert_2'=2] {'expert_0','expert_..., use_global_device_ids=true, to_apply=%region_3.4 | all-reduce | flops 1024 | bytes 8192 | tf_op jit(solution)/shard_map/psum | solution.py:37
  145.9 0.1 select_reduce_fusion.2
  146.1 13.5 %psum.15 = s32[8,32]{1,0:T(8,128)S(1)} all-reduce(s32[8,32]{1,0:T(8,128)S(1)} %broadcast_select_fusion.1), channel_id=1, replica_groups=mesh['dp'=8,'expert_0'=4,'expert_1'=4,'expert_2'=2] {'dp'}, use_global_device_ids=true, to_apply=%region_5.6 | all-reduce | flops 256 | bytes 2048 | tf_op jit(solution)/shard_map/psum | solution.py:39
  159.6 0.7 reduce_max.9
  161.0 0.1 copy.25
  161.2 10.9 %all-gather = f32[1,1024]{1,0:T(1,128)S(1)} all-gather(f32[1,128]{1,0:T(1,128)S(1)} %copy-done.1), channel_id=2, replica_groups=mesh['dp'=8,'expert_0'=4,'expert_1'=4,'expert_2'=2] {'dp'}, dimensions={1}, use_global_device_ids=true | all-gather | bytes 4608 | tf_op jit(solution)/shard_map/all_gather | solution.py:50
  172.1 155.2 %conditional.2 = (bf16[256,2048]{1,0:T(8,128)(2,1)S(1)}) conditional(s32[]{:T(128)} %convert_element_type.51, (s32[32]{0:T(128)S(1)}, s32[32,8]{1,0:T(8,128)S(1)}, s32[32,1]{1,0:T(8,128)S(1)}, s32[32,8]{1,0:T(8,128)S(1)}, f32[1024]{0:T(1024)S(1)}, /*index=5*/s32[]{:T(128)}, s32[8]{0:T(128)S(1)}, pred[32]{0:T(512)(128)(4,1)S(1)}, ...), branch_computations={%region_9.12_spmd, %region_12.15_spmd} | conditional | flops 17727356928 | bytes 85999704
  172.3 0.1 eq.45
  172.4 1.3 convolution_convert_fusion.3
  173.7 0.2 reduce-scatter.5.cloned.1.call-start
  174.0 70.5 %all-gather.6.cloned.1.call-done = bf16[1280,2048]{1,0:T(8,128)(2,1)} async-done(((bf16[160,2048]{1,0:T(8,128)(2,1)}), bf16[1280,2048]{1,0:T(8,128)(2,1)}) %all-gather.6.cloned.1.call-update) | async-done | bytes 5242896 | tf_op jit(solution)/shard_map/cond/branch_1_fun/all_gather | solution.py:59
  244.4 16.9 %convolution_convert_fusion.2 = bf16[1280,2048]{1,0:T(8,128)(2,1)} fusion(bf16[1,1024,2048]{2,1,0:T(8,128)(2,1)} %get-tuple-element.129, bf16[1280,2048]{1,0:T(8,128)(2,1)} %all-gather.6.cloned.1.call-done, bf16[1,2048,1024]{2,1,0:T(8,128)(2,1)} %get-tuple-element.128), kind=kOutput, calls=%fused_computation.19 | convolution fusion | flops 10742661120 | bytes 18874368 | tf_op jit(solution)/shard_map/cond/branch_1_fun/dot_general | solution.py:63
  261.4 0.7 select_reduce_fusion.1
  264.1 61.4 %reduce-scatter.5.cloned.1.call-done = bf16[160,2048]{1,0:T(8,128)(2,1)} async-done(((bf16[1280,2048]{1,0:T(8,128)(2,1)}), bf16[160,2048]{1,0:T(8,128)(2,1)}) %reduce-scatter.5.cloned.1.call-update) | async-done | bytes 655376 | tf_op jit(solution)/shard_map/cond/branch_1_fun/reduce_scatter | solution.py:64
  325.4 1.6 fusion.15
  327.3 24.3 %all_to_all.10 = bf16[32,8,2048]{2,1,0:T(8,128)(2,1)S(1)} all-to-all(bf16[32,8,2048]{2,1,0:T(8,128)(2,1)S(1)} %bitcast.60), channel_id=1, replica_groups=mesh['dp'=8,'expert_0'=4,'expert_1'=4,'expert_2'=2] {'expert_0','expert_..., dimensions={0} | all-to-all | bytes 2097152 | tf_op jit(solution)/shard_map/all_to_all | solution.py:79
  351.5 1.5 fusion.20
  (25 shorter events, 0.6 us)
Async XLA Ops:
  6.5 2.0 copy-start
  6.5 154.6 %copy-start.1 = (f32[1,128]{1,0:T(1,128)S(1)}, f32[1,128]{1,0:T(1,128)}, u32[]{:S(2)}) copy-start(f32[1,128]{1,0:T(1,128)} %param.13) | copy-start | bytes 1540
  10.0 162.1 %all-to-all-start = ((bf16[32,8,2048]{2,1,0:T(8,128)(2,1)}), bf16[32,8,2048]{2,1,0:T(8,128)(2,1)S(1)}, u32[]{:S(2)}, u32[]{:S(2)}) async-start(bf16[32,8,2048]{2,1,0:T(8,128)(2,1)} %fusion.21), calls=%async_computation.2 | async-start | bytes 2097152 | tf_op jit(solution)/shard_map/all_to_all | solution.py:32
  172.1 72.3 %all-gather.6.cloned.1.call-start = ((), (), s32[]{:S(2)}) async-start(), calls=%async_computation.6 | async-start | bytes 5898240 | tf_op jit(solution)/shard_map/cond/branch_1_fun/all_gather | solution.py:59
  173.7 151.7 %reduce-scatter.5.cloned.1.call-start = ((), (), s32[]{:S(2)}) async-start(), calls=%async_computation.7 | async-start | bytes 5898240 | tf_op jit(solution)/shard_map/cond/branch_1_fun/reduce_scatter | solution.py:64
Sparse Core Ops, SparseCore 0:
  174.7 69.7 all-gather.5
  261.5 63.9 reduce-scatter.4
where the time goes:
time: 360 us
  blocking collectives  176 us (49%)
  waiting for transfers between devices  132 us (37%)
  matrix products  22.7 us (6%)
  between operations  14.1 us (4%)
  starting transfers between devices  8.84 us (2%)
    psum x1, blocking collectives, on_device(): lax.psum(jnp.where(device_ids == own_expert, counts[None, :], 0), EXPERT)  127 us
    all_gather x1, waiting for transfers between devices, experts(): slot_rows = lax.all_gather(plane, 'dp', axis=0, tiled=True)  70.5 us
    reduce_scatter x1, waiting for transfers between devices, experts(): lax.psum_scatter(share.astype(jnp.bfloat16), 'dp', scatter_dimension=0, t...  61.4 us
    all_to_all x1, blocking collectives, on_device(): lax.all_to_all(sent_back.reshape(expert_count, MOST, width), EXPERT, spli...  24.3 us
    dot_general x1, matrix products, experts(): share = jnp.dot(hidden, weight_out[0], preferred_element_type=jnp.float32)  16.9 us
    psum x1, blocking collectives, on_device(): lax.psum(jnp.where(plane_ids == own_dp, jnp.sum(table, axis=0)[None, :],...  13.5 us
    all_gather x1, blocking collectives, on_device(): gates_all = lax.all_gather(gate_weights[0], 'dp', axis=0, tiled=True)  10.9 us
    all_to_all x1, starting transfers between devices, on_device(): lax.all_to_all(packed.reshape(expert_count, MOST, width), EXPERT, split_a...  8.58 us
  transfers between devices with their start and end apart: 3, of which 2 were waited for; matrix products, arithmetic and copies ran while one was open for 1% of the time, Pallas kernels for 0%

commit v1 on v0

--- a/solution.py
+++ b/solution.py
@@ -56,7 +56,10 @@
         plane = lax.dot_general(
             place_table, rows, (((0,), (0,)), ((), ())), preferred_element_type=jnp.float32
         ).astype(jnp.bfloat16)
-        slot_rows = lax.all_gather(plane, "dp", axis=0, tiled=True)
+        count = lax.axis_size("dp")
+        blocks = jnp.stack([plane for _ in range(count)])
+        blocks = lax.all_to_all(blocks, "dp", split_axis=0, concat_axis=0)
+        slot_rows = jnp.concatenate(blocks, axis=0)
         hidden = jnp.maximum(
             jnp.dot(slot_rows, weight_in[0], preferred_element_type=jnp.float32), 0.0
         ).astype(jnp.bfloat16)

time: 360 us -> 409 us (1.14)
  blocking collectives: 176 us -> 286 us
  waiting for transfers between devices: 132 us -> 71 us
    all_to_all x0 -> x1, blocking collectives: none -> 110 us  [experts(): blocks = lax.all_to_all(blocks, 'dp', split_axis=0, concat_axis=0)]
    all_gather x1 -> x0, waiting for transfers between devices: 70.5 us -> none  [experts(): slot_rows = lax.all_gather(plane, 'dp', axis=0, tiled=True)]
    reduce_scatter x1, waiting for transfers between devices: 61.4 us -> 71 us  [experts(): lax.psum_scatter(share.astype(jnp.bfloat16), 'dp', scatter_dimension=0, t...]
  transfers between devices with their start and end apart: 3 -> 2, of which waited for: 2 -> 1; matrix products, arithmetic and copies ran while one was open for 1% -> 0% of each run, Pallas kernels for 0% -> 0%
where the time goes in v1:
time: 409 us
  blocking collectives  286 us (70%)
  waiting for transfers between devices  71 us (17%)
  matrix products  21.9 us (5%)
  between operations  14.1 us (3%)
  starting transfers between devices  8.62 us (2%)
    psum x1, blocking collectives, on_device(): lax.psum(jnp.where(device_ids == own_expert, counts[None, :], 0), EXPERT)  127 us
    all_to_all x1, blocking collectives, experts(): blocks = lax.all_to_all(blocks, 'dp', split_axis=0, concat_axis=0)  110 us
    reduce_scatter x1, waiting for transfers between devices, experts(): lax.psum_scatter(share.astype(jnp.bfloat16), 'dp', scatter_dimension=0, t...  71 us
    all_to_all x1, blocking collectives, on_device(): lax.all_to_all(sent_back.reshape(expert_count, MOST, width), EXPERT, spli...  24.3 us
    dot_general x1, matrix products, experts(): share = jnp.dot(hidden, weight_out[0], preferred_element_type=jnp.float32)  16.9 us
    psum x1, blocking collectives, on_device(): lax.psum(jnp.where(plane_ids == own_dp, jnp.sum(table, axis=0)[None, :],...  13.5 us
    all_gather x1, blocking collectives, on_device(): gates_all = lax.all_gather(gate_weights[0], 'dp', axis=0, tiled=True)  10.9 us
    all_to_all x1, starting transfers between devices, on_device(): lax.all_to_all(packed.reshape(expert_count, MOST, width), EXPERT, split_a...  8.58 us
  transfers between devices with their start and end apart: 2, of which 1 were waited for; matrix products, arithmetic and copies ran while one was open for 0% of the time, Pallas kernels for 0%

profile of v1, /device:TPU:1, one launch (start us, length us, event | category | flops | bytes accessed | tf_op | source)
XLA Modules:
  0.0 408.7 jit_solution(16161367549824904006)
XLA Ops:
  6.5 0.9 convert_bitcast_fusion.1
  7.5 0.6 reduce-window.11
  8.1 0.2 slice_reduce_fusion
  8.3 0.1 iota.68
  8.4 0.1 convert_subtract_fusion
  8.5 1.5 fusion.21
  10.0 8.6 %all-to-all-start.2 = ((bf16[32,8,2048]{2,1,0:T(8,128)(2,1)}), bf16[32,8,2048]{2,1,0:T(8,128)(2,1)S(1)}, u32[]{:S(2)}, u32[]{:S(2)}) async-start(bf16[32,8,2048]{2,1,0:T(8,128)(2,1)} %fusion.21), calls=%async_computation.4 | async-start | bytes 2097152 | tf_op jit(solution)/shard_map/all_to_all | solution.py:32
  18.7 127.2 %psum.14 = s32[32,32]{1,0:T(8,128)S(1)} all-reduce(s32[32,32]{1,0:T(8,128)S(1)} %broadcast_select_fusion), channel_id=1, replica_groups=mesh['dp'=8,'expert_0'=4,'expert_1'=4,'expert_2'=2] {'expert_0','expert_..., use_global_device_ids=true, to_apply=%region_3.4 | all-reduce | flops 1024 | bytes 8192 | tf_op jit(solution)/shard_map/psum | solution.py:37
  145.9 0.1 select_reduce_fusion.2
  146.1 13.5 %psum.15 = s32[8,32]{1,0:T(8,128)S(1)} all-reduce(s32[8,32]{1,0:T(8,128)S(1)} %broadcast_select_fusion.1), channel_id=1, replica_groups=mesh['dp'=8,'expert_0'=4,'expert_1'=4,'expert_2'=2] {'dp'}, use_global_device_ids=true, to_apply=%region_5.6 | all-reduce | flops 256 | bytes 2048 | tf_op jit(solution)/shard_map/psum | solution.py:39
  159.6 0.7 reduce_max.9
  161.0 0.1 copy.25
  161.2 10.9 %all-gather = f32[1,1024]{1,0:T(1,128)S(1)} all-gather(f32[1,128]{1,0:T(1,128)S(1)} %copy-done.1), channel_id=2, replica_groups=mesh['dp'=8,'expert_0'=4,'expert_1'=4,'expert_2'=2] {'dp'}, dimensions={1}, use_global_device_ids=true | all-gather | bytes 4608 | tf_op jit(solution)/shard_map/all_gather | solution.py:50
  172.1 204.0 %conditional.2 = (bf16[256,2048]{1,0:T(8,128)(2,1)S(1)}) conditional(s32[]{:T(128)} %convert_element_type.51, (s32[32]{0:T(128)S(1)}, s32[32,8]{1,0:T(8,128)S(1)}, s32[32,1]{1,0:T(8,128)S(1)}, s32[32,8]{1,0:T(8,128)S(1)}, f32[1024]{0:T(1024)S(1)}, /*index=5*/s32[]{:T(128)}, s32[8]{0:T(128)S(1)}, pred[32]{0:T(512)(128)(4,1)S(1)}, ...), branch_computations={%region_9.12_spmd, %region_12.15_spmd} | conditional | flops 17727356928 | bytes 83902504
  172.3 0.1 eq.45
  172.4 0.5 convolution_convert_fusion.3
  172.9 0.7 stack.2
  173.5 110.1 %all_to_all.19 = bf16[8,160,2048]{2,1,0:T(8,128)(2,1)} all-to-all(bf16[8,160,2048]{2,1,0:T(8,128)(2,1)S(1)} %stack.2), channel_id=1, replica_groups=mesh['dp'=8,'expert_0'=4,'expert_1'=4,'expert_2'=2] {'dp'}, dimensions={0} | all-to-all | bytes 10485760 | tf_op jit(solution)/shard_map/cond/branch_1_fun/all_to_all | solution.py:61
  283.6 16.9 %convolution_convert_fusion.2 = bf16[1280,2048]{1,0:T(8,128)(2,1)} fusion(bf16[1,1024,2048]{2,1,0:T(8,128)(2,1)} %get-tuple-element.129, bf16[1280,2048]{1,0:T(8,128)(2,1)} %bitcast.63, bf16[1,2048,1024]{2,1,0:T(8,128)(2,1)} %get-tuple-element.128), kind=kOutput, calls=%fused_computation.19 | convolution fusion | flops 10742661120 | bytes 18874368 | tf_op jit(solution)/shard_map/cond/branch_1_fun/dot_general | solution.py:66
  300.5 0.7 select_reduce_fusion.1
  303.3 71.0 %reduce-scatter.5.cloned.1.call-done = bf16[160,2048]{1,0:T(8,128)(2,1)} async-done(((bf16[1280,2048]{1,0:T(8,128)(2,1)}), bf16[160,2048]{1,0:T(8,128)(2,1)}) %reduce-scatter.5.cloned.1.call-update) | async-done | bytes 655376 | tf_op jit(solution)/shard_map/cond/branch_1_fun/reduce_scatter | solution.py:67
  374.2 1.6 fusion.15
  376.1 24.3 %all_to_all.20 = bf16[32,8,2048]{2,1,0:T(8,128)(2,1)S(1)} all-to-all(bf16[32,8,2048]{2,1,0:T(8,128)(2,1)S(1)} %bitcast.64), channel_id=1, replica_groups=mesh['dp'=8,'expert_0'=4,'expert_1'=4,'expert_2'=2] {'expert_0','expert_..., dimensions={0} | all-to-all | bytes 2097152 | tf_op jit(solution)/shard_map/all_to_all | solution.py:82
  400.3 1.5 fusion.20
  (24 shorter events, 0.6 us)
Async XLA Ops:
  6.5 2.0 copy-start
  6.5 154.6 %copy-start.1 = (f32[1,128]{1,0:T(1,128)S(1)}, f32[1,128]{1,0:T(1,128)}, u32[]{:S(2)}) copy-start(f32[1,128]{1,0:T(1,128)} %param.13) | copy-start | bytes 1540
  10.0 162.1 %all-to-all-start.2 = ((bf16[32,8,2048]{2,1,0:T(8,128)(2,1)}), bf16[32,8,2048]{2,1,0:T(8,128)(2,1)S(1)}, u32[]{:S(2)}, u32[]{:S(2)}) async-start(bf16[32,8,2048]{2,1,0:T(8,128)(2,1)} %fusion.21), calls=%async_computation.4 | async-start | bytes 2097152 | tf_op jit(solution)/shard_map/all_to_all | solution.py:32
  172.1 202.2 %reduce-scatter.5.cloned.1.call-start = ((), (), s32[]{:S(2)}) async-start(), calls=%async_computation.7 | async-start | bytes 5898240 | tf_op jit(solution)/shard_map/cond/branch_1_fun/reduce_scatter | solution.py:67
Sparse Core Ops, SparseCore 0:
  300.6 73.5 reduce-scatter.4
